TPU v7x, 32 devices: a whole 2x2x4 slice. The times are simulated.
32 devices in a mesh: rep: 4 (over y, x), tile: 8 (over z, core).
Axes of the slice: x: 2, y: 2, z: 4, core: 2. Of those that a mesh axis runs over, the one named last changes fastest.
Arguments:
- spins_in: float32 [4, 2048, 4096], P('rep', 'tile'), may hold values from -1 to 1
- noise: bfloat16 [2, 4, 2048, 4096], P(None, 'rep', 'tile'), may hold values from -1.5 to 1.5
- betas: float32 [4], replicated, as said below
- labels: int32 [4], P('rep'), may hold values from 0 to 3, each once
- accept: int32 [2, 4], P(None, 'rep'), may hold values 0 or 1
Outputs:
- spins: float32 [4, 2048, 4096], P('rep', 'tile')
- energy_rows: float32 [4, 2048], P('rep', 'tile')
- margin_rows: float32 [4, 2048], P('rep', 'tile')
- new_labels: int32 [4], P('rep')
- log_ratio: float32 [4], P('rep')
- new_beta: float32 [4], P('rep')
Inputs may be any that keep to these rules, and one draw needn't show every extreme that they name: `labels`: a permutation of the temperature indices. `accept`: entry [p, r] is read only where r mod 2 equals p. `betas`: distinct and positive.
All inputs are finite; a program needn't handle non-finite values. No bound on the sum of `accept` on one device may be relied on, other than what follows from the above.
Results may differ from a plain program's by a relative error of at most 0.0003.
Values sent between devices are 32-bit elements; how exact they have to be, the bound alone decides.
A program may use at most 64 MiB of HBM per device.

v0:
```python
import jax
import jax.numpy as jnp
from jax import lax
from jax.sharding import PartitionSpec as P

SWEEPS = 2


def padded_2(value, sides, width):
    for axis, dim in sides:
        peers, length = (lax.axis_size(axis), value.shape[dim])
        up = [(i, (i + 1) % peers) for i in range(peers)]
        down = [(j, i) for i, j in up]
        last = lax.slice_in_dim(value, length - width, length, axis=dim)
        leading = lax.slice_in_dim(value, 0, width, axis=dim)
        before = lax.ppermute(last, axis, up)
        after = lax.ppermute(leading, axis, down)
        value = jnp.concatenate([before, value, after], axis=dim)
    return value


def shifted(value, axis, by):
    peers = lax.axis_size(axis)
    return lax.ppermute(value, axis, [(i, (i + by) % peers) for i in range(peers)])


def ladder(energy, labels, accept, betas):
    count = energy.shape[0]
    slots = jnp.arange(count, dtype=jnp.int32)
    even = slots % 2 == 0
    accept_zero = accept[0]
    accept_one = accept[1]

    def beta_of(label_set):
        return jnp.sum(jnp.where(label_set[:, None] == slots[None, :], betas[None, :], 0.0), axis=1)

    e_next = jnp.roll(energy, -1)
    beta_zero = beta_of(labels)
    log_zero = (beta_zero - jnp.roll(beta_zero, -1)) * (energy - e_next)
    swap_zero = jnp.where(even, accept_zero, jnp.roll(accept_zero, 1))
    labels_one = jnp.where(
        swap_zero == 1, jnp.where(even, jnp.roll(labels, -1), jnp.roll(labels, 1)), labels
    )
    beta_one = beta_of(labels_one)
    log_one = (beta_one - jnp.roll(beta_one, -1)) * (energy - e_next)
    swap_one = jnp.where(even, jnp.roll(accept_one, 1), accept_one)
    labels_two = jnp.where(
        swap_one == 1,
        jnp.where(even, jnp.roll(labels_one, 1), jnp.roll(labels_one, -1)),
        labels_one,
    )
    return (labels_two, jnp.where(even, log_zero, log_one), beta_of(labels_two))


def padded_rows(lattice):
    return padded_2(lattice, (("tile", 0),), 1)


def colour_of(count_rows, cols):
    return (
        lax.broadcasted_iota(jnp.int32, (count_rows, cols), 0)
        + lax.broadcasted_iota(jnp.int32, (count_rows, cols), 1)
    ) % 2


def body(spins_in, noise, betas, labels, accept):
    lattice = spins_in[0]
    rows, cols = lattice.shape
    count = betas.shape[0]
    slots_float = jnp.arange(count, dtype=jnp.float32)
    label_float = labels.astype(jnp.float32)
    accept_zero = accept[0].astype(jnp.float32)
    accept_one = accept[1].astype(jnp.float32)
    beta = jnp.sum(jnp.where(slots_float == label_float[0], betas, 0.0))
    parity = colour_of(rows, cols)
    for sweep in range(SWEEPS):
        for colour in range(2):
            padded = padded_rows(lattice)
            field = padded[:-2] + padded[2:] + jnp.roll(lattice, 1, 1) + jnp.roll(lattice, -1, 1)
            fresh = jnp.tanh(beta * field + noise[sweep, 0].astype(jnp.float32))
            lattice = jnp.where(parity == colour, fresh, lattice)
    padded = padded_rows(lattice)
    below = padded[2:]
    row_energy = -jnp.mean(lattice * (below + jnp.roll(lattice, -1, 1)), axis=1)
    total = lax.psum(jnp.sum(row_energy), "tile")
    energy = jnp.reshape(total / (rows * lax.axis_size("tile")), (1,))
    half = rows // 2
    upper = shifted(lattice[:half], "rep", -1)
    margin_upper = jnp.mean(lattice[:half] * upper, axis=1)
    lower = shifted(lattice[half:], "rep", 1)
    lower_here = jnp.mean(lower * lattice[half:], axis=1)
    margin_lower = shifted(lower_here, "rep", -1)
    margin = jnp.concatenate([margin_upper, margin_lower], axis=0)
    slot = lax.axis_index("rep")
    accept_pair = jnp.concatenate([accept_zero, accept_one], axis=0)
    energies, label_all, accept_all = (
        lax.all_gather(energy, "rep", axis=0, tiled=True),
        lax.all_gather(label_float, "rep", axis=0, tiled=True),
        lax.all_gather(accept_pair, "rep", axis=0, tiled=True),
    )
    accept_rows = jnp.transpose(jnp.reshape(accept_all, (count, 2))).astype(jnp.int32)
    label_set, log_set, beta_set = ladder(energies, label_all.astype(jnp.int32), accept_rows, betas)
    new_labels = lax.dynamic_slice_in_dim(label_set, slot, 1)
    log_ratio = lax.dynamic_slice_in_dim(log_set, slot, 1)
    new_beta = lax.dynamic_slice_in_dim(beta_set, slot, 1)
    return (lattice[None], row_energy[None], margin[None], new_labels, log_ratio, new_beta)


def solution(mesh):
    in_specs = (P("rep", "tile", None), P(None, "rep", "tile", None), P(), P("rep"), P(None, "rep"))
    out_specs = (
        P("rep", "tile", None),
        P("rep", "tile"),
        P("rep", "tile"),
        P("rep"),
        P("rep"),
        P("rep"),
    )
    return jax.shard_map(body, mesh=mesh, in_specs=in_specs, out_specs=out_specs, check_vma=False)
```

profile of v0, /device:TPU:0, one launch (start us, length us, event | category | flops | bytes accessed | tf_op | source)
XLA Modules:
  0.0 191.1 jit_solution(809667553719057791)
XLA Ops:
  2.2 4.1 %collective-permute-start.1 = (f32[1,4096]{1,0:T(1,128)S(1)}, f32[1,4096]{1,0:T(1,128)S(1)}, u32[]{:S(2)}, u32[]{:S(2)}) collective-permute-start(f32[1,4096]{1,0:T(1,128)S(1)} %get-tuple-element.43), channel_id=1, source_target_pairs={{1,0},{2,1},{3,2},{4,3},{5,4},{6,5},{7,6},{0,7},{9,8},{10,9},{11,1... | collective-permute-start | bytes 49160 | tf_op jit(solution)/shard_map/ppermute | solution.py:17
  6.3 8.1 %fusion.46 = (f32[256,4095]{1,0:T(8,128)}, f32[256,4095]{1,0:T(8,128)}) fusion(f32[256,4096]{1,0:T(8,128)} %bitcast.29), kind=kLoop, calls=%fused_computation.96 | loop fusion | bytes 16773120 | tf_op jit(solution)/shard_map/jit(_roll_static)/slice | solution.py:79
  20.0 11.3 %fusion.1 = f32[256,4096]{1,0:T(8,128)S(1)} fusion(f32[256,4096]{1,0:T(8,128)} %bitcast.31, f32[1,4096]{1,0:T(1,128)S(1)} %collective-permute-done.1, f32[1,4096]{1,0:T(1,128)S(1)} %collective-permute-done, f32[256,4095]{1,0:T(8,128)} %get-tuple-element.39, f32[256,1]{1,0:T(8,128)S(1)} %get-tuple-element.41, f32[256,1]{1,0:T(8,128)S(1)} %get-tuple-element.40, ...), kind=kLoop, calls=%fused_computation.8 | loop fusion | flops 25165824 | bytes 18907140 | tf_op jit(solution)/shard_map/jit(_where)/select_n | solution.py:81
  31.3 1.6 fusion.43
  32.9 3.5 %collective-permute-start.3 = (f32[1,4096]{1,0:T(1,128)S(1)}, f32[1,4096]{1,0:T(1,128)S(1)}, u32[]{:S(2)}, u32[]{:S(2)}) collective-permute-start(f32[1,4096]{1,0:T(1,128)S(1)} %get-tuple-element.37), channel_id=1, source_target_pairs={{1,0},{2,1},{3,2},{4,3},{5,4},{6,5},{7,6},{0,7},{9,8},{10,9},{11,1... | collective-permute-start | bytes 49160 | tf_op jit(solution)/shard_map/ppermute | solution.py:17
  36.6 1.3 collective-permute-done.2
  37.9 7.3 %fusion.3 = f32[256,4096]{1,0:T(8,128)S(1)} fusion(f32[256,4096]{1,0:T(8,128)S(1)} %fusion.1, f32[1,4096]{1,0:T(1,128)S(1)} %collective-permute-done.3, f32[1,4096]{1,0:T(1,128)S(1)} %collective-permute-done.2, f32[256,4095]{1,0:T(8,128)S(1)} %get-tuple-element.33, f32[256,1]{1,0:T(8,128)S(1)} %get-tuple-element.35, f32[256,1]{1,0:T(8,128)S(1)} %get-tuple-element.34, ...), kind=kLoop, calls=%fused_computation.10 | loop fusion | flops 25165824 | bytes 18907140 | tf_op jit(solution)/shard_map/jit(_where)/select_n | solution.py:81
  45.2 1.6 fusion.40
  46.9 3.8 %collective-permute-start.5 = (f32[1,4096]{1,0:T(1,128)S(1)}, f32[1,4096]{1,0:T(1,128)S(1)}, u32[]{:S(2)}, u32[]{:S(2)}) collective-permute-start(f32[1,4096]{1,0:T(1,128)S(1)} %get-tuple-element.31), channel_id=1, source_target_pairs={{1,0},{2,1},{3,2},{4,3},{5,4},{6,5},{7,6},{0,7},{9,8},{10,9},{11,1... | collective-permute-start | bytes 49160 | tf_op jit(solution)/shard_map/ppermute | solution.py:17
  52.1 7.3 %fusion.5 = f32[256,4096]{1,0:T(8,128)S(1)} fusion(f32[256,4096]{1,0:T(8,128)S(1)} %fusion.3, f32[1,4096]{1,0:T(1,128)S(1)} %collective-permute-done.5, f32[1,4096]{1,0:T(1,128)S(1)} %collective-permute-done.4, f32[256,4095]{1,0:T(8,128)S(1)} %get-tuple-element.27, f32[256,1]{1,0:T(8,128)S(1)} %get-tuple-element.29, f32[256,1]{1,0:T(8,128)S(1)} %get-tuple-element.28, ...), kind=kLoop, calls=%fused_computation.12 | loop fusion | flops 25165824 | bytes 18907140 | tf_op jit(solution)/shard_map/jit(_where)/select_n | solution.py:81
  59.3 1.6 fusion.37
  61.0 3.6 %collective-permute-start.7 = (f32[1,4096]{1,0:T(1,128)S(1)}, f32[1,4096]{1,0:T(1,128)S(1)}, u32[]{:S(2)}, u32[]{:S(2)}) collective-permute-start(f32[1,4096]{1,0:T(1,128)S(1)} %get-tuple-element.25), channel_id=1, source_target_pairs={{1,0},{2,1},{3,2},{4,3},{5,4},{6,5},{7,6},{0,7},{9,8},{10,9},{11,1... | collective-permute-start | bytes 49160 | tf_op jit(solution)/shard_map/ppermute | solution.py:17
  64.7 1.3 collective-permute-done.6
  66.0 7.2 %fusion.7 = f32[256,4096]{1,0:T(8,128)S(1)} fusion(f32[256,4096]{1,0:T(8,128)S(1)} %fusion.5, f32[1,4096]{1,0:T(1,128)S(1)} %collective-permute-done.7, f32[1,4096]{1,0:T(1,128)S(1)} %collective-permute-done.6, f32[256,4095]{1,0:T(8,128)S(1)} %get-tuple-element.21, f32[256,1]{1,0:T(8,128)S(1)} %get-tuple-element.23, f32[256,1]{1,0:T(8,128)S(1)} %get-tuple-element.22, ...), kind=kLoop, calls=%fused_computation.14 | loop fusion | flops 25165824 | bytes 18907140 | tf_op jit(solution)/shard_map/jit(_where)/select_n | solution.py:81
  73.3 3.6 %collective-permute-start.8 = (f32[1,4096]{1,0:T(1,128)S(1)}, f32[1,4096]{1,0:T(1,128)S(1)}, u32[]{:S(2)}, u32[]{:S(2)}) collective-permute-start(f32[1,4096]{1,0:T(1,128)S(1)} %slice.321), channel_id=1, source_target_pairs={{1,0},{2,1},{3,2},{4,3},{5,4},{6,5},{7,6},{0,7},{9,8},{10,9},{11,1... | collective-permute-start | bytes 49160 | tf_op jit(solution)/shard_map/ppermute | solution.py:17
  76.8 2.4 %fusion.36 = (f32[128,4096]{1,0:T(8,128)}, f32[128,4096]{1,0:T(8,128)}) fusion(f32[256,4096]{1,0:T(8,128)S(1)} %fusion.7), kind=kLoop, calls=%fused_computation.86 | loop fusion | bytes 8388608 | tf_op jit(solution)/shard_map/slice | solution.py:90
  80.4 2.0 %collective-permute-start.10 = (f32[128,4096]{1,0:T(8,128)}, f32[128,4096]{1,0:T(8,128)S(1)}, u32[]{:S(2)}, u32[]{:S(2)}) collective-permute-start(f32[128,4096]{1,0:T(8,128)} %get-tuple-element.18), channel_id=1, source_target_pairs={{0,8},{8,16},{16,24},{24,0},{1,9},{9,17},{17,25},{25,1},{2,10},{10... | collective-permute-start | bytes 6291464 | tf_op jit(solution)/shard_map/ppermute | solution.py:24
  86.8 14.2 %psum.7 = f32[]{:T(128)} all-reduce(f32[]{:T(128)S(6)} %neg.17), channel_id=1, replica_groups=mesh['rep'=4,'tile'=8] {'tile'}, use_global_device_ids=true, to_apply=%region_6.7 | all-reduce | flops 1 | bytes 8 | tf_op jit(solution)/shard_map/psum | solution.py:85
  102.5 72.4 %all-reduce.3 = (f32[8]{0:T(128)S(1)}, f32[4]{0:T(128)S(1)}, f32[4]{0:T(128)S(1)}) all-reduce(f32[8]{0:T(128)S(1)} %maximum_dynamic-update-slice_fusion, f32[4]{0:T(128)S(1)} %convert_dynamic-update-slice_fusion, f32[4]{0:T(128)S(1)} %dynamic-update-slice.2), channel_id=1, replica_groups=mesh['rep'=4,'tile'=8] {'rep'}, use_global_device_ids=true, to_apply=%add | all-reduce | flops 16 | bytes 128
  176.5 2.0 %compare_select_fusion = s32[4]{0:T(128)S(1)} fusion(s32[4]{0:T(128)S(1)} %get-tuple-element.11, s32[3]{0:T(128)S(1)} %get-tuple-element.9, s32[1]{0:T(128)} %bitcast.14, s32[1]{0:T(128)} %get-tuple-element.53, s32[3]{0:T(128)S(1)} %get-tuple-element.55, s32[3]{0:T(128)S(1)} %get-tuple-element.54, s32[1]{0:T(128)} %get-tuple-element.52, ...), kind=kLoop, calls=%fused_computation.63 | loop fusion | flops 60 | bytes 96 | tf_op jit(solution)/shard_map/jit(_where)/select_n | solution.py:41
  179.2 2.0 %compare_select_fusion.1 = s32[4]{0:T(128)S(1)} fusion(s32[4]{0:T(128)S(1)} %compare_select_fusion, s32[4]{0:T(128)S(1)} %get-tuple-element.10, s32[3]{0:T(128)S(1)} %get-tuple-element.8, s32[1]{0:T(128)} %bitcast.13, s32[3]{0:T(128)S(1)} %get-tuple-element.49, s32[1]{0:T(128)} %get-tuple-element.51, s32[1]{0:T(128)} %get-tuple-element.50, ...), kind=kLoop, calls=%fused_computation.64 | loop fusion | flops 56 | bytes 96 | tf_op jit(solution)/shard_map/jit(_where)/select_n | solution.py:47
  183.5 3.3 %multiply_reduce_fusion.1 = (f32[128]{0:T(128)S(1)}, f32[128]{0:T(128)S(1)}) fusion(f32[128,4096]{1,0:T(8,128)} %collective-permute-done.9, f32[256,4096]{1,0:T(8,128)} %copy-done, f32[128,4096]{1,0:T(8,128)S(1)} %collective-permute-done.10), kind=kLoop, calls=%fused_computation.48 | loop fusion | flops 2096896 | bytes 8389632 | tf_op jit(solution)/shard_map/reduce_sum | solution.py:89
  186.9 1.5 collective-permute-start.11
  188.4 2.1 %collective-permute-done.11 = f32[128]{0:T(128)S(1)} collective-permute-done((f32[128]{0:T(128)S(1)}, f32[128]{0:T(128)S(1)}, u32[]{:S(2)}, u32[]{:S(2)}) %collective-permute-start.11) | collective-permute-done | bytes 544 | tf_op jit(solution)/shard_map/ppermute | solution.py:24
  (67 shorter events, 17.5 us)
Async XLA Ops:
  1.6 18.4 %collective-permute-start = (f32[1,4096]{1,0:T(1,128)S(1)}, f32[1,4096]{1,0:T(1,128)S(1)}, u32[]{:S(2)}, u32[]{:S(2)}) collective-permute-start(f32[1,4096]{1,0:T(1,128)S(1)} %get-tuple-element.42), channel_id=1, source_target_pairs={{0,1},{1,2},{2,3},{3,4},{4,5},{5,6},{6,7},{7,0},{8,9},{9,10},{10,1... | collective-permute-start | bytes 49160 | tf_op jit(solution)/shard_map/ppermute | solution.py:16
  2.2 17.8 %collective-permute-start.1 = (f32[1,4096]{1,0:T(1,128)S(1)}, f32[1,4096]{1,0:T(1,128)S(1)}, u32[]{:S(2)}, u32[]{:S(2)}) collective-permute-start(f32[1,4096]{1,0:T(1,128)S(1)} %get-tuple-element.43), channel_id=1, source_target_pairs={{1,0},{2,1},{3,2},{4,3},{5,4},{6,5},{7,6},{0,7},{9,8},{10,9},{11,1... | collective-permute-start | bytes 49160 | tf_op jit(solution)/shard_map/ppermute | solution.py:17
  6.3 9.8 %copy-start.2 = (s32[2,1]{0,1:T(1,128)S(1)}, s32[2,1]{0,1:T(1,128)}, u32[]{:S(2)}) copy-start(s32[2,1]{0,1:T(1,128)} %param.9) | copy-start | bytes 28
  6.3 11.7 %copy-start.3 = (f32[4]{0:T(128)S(1)}, f32[4]{0:T(128)}, u32[]{:S(2)}) copy-start(f32[4]{0:T(128)} %param.7) | copy-start | bytes 52
  6.3 12.3 %copy-start.4 = (u32[32]{0:T(128)S(1)}, u32[32]{0:T(128)}, u32[]{:S(2)}) copy-start(u32[32]{0:T(128)} %constant.53) | copy-start | bytes 388
  31.3 6.6 %copy-start.1 = (bf16[2,1,256,4096]{3,2,1,0:T(8,128)(2,1)S(1)}, bf16[2,1,256,4096]{3,2,1,0:T(8,128)(2,1)}, u32[]{:S(2)}) copy-start(bf16[2,1,256,4096]{3,2,1,0:T(8,128)(2,1)} %param.6) | copy-start | bytes 12582916
  32.9 5.0 %collective-permute-start.2 = (f32[1,4096]{1,0:T(1,128)S(1)}, f32[1,4096]{1,0:T(1,128)S(1)}, u32[]{:S(2)}, u32[]{:S(2)}) collective-permute-start(f32[1,4096]{1,0:T(1,128)S(1)} %get-tuple-element.36), channel_id=1, source_target_pairs={{0,1},{1,2},{2,3},{3,4},{4,5},{5,6},{6,7},{7,0},{8,9},{9,10},{10,1... | collective-permute-start | bytes 49160 | tf_op jit(solution)/shard_map/ppermute | solution.py:16
  32.9 5.0 %collective-permute-start.3 = (f32[1,4096]{1,0:T(1,128)S(1)}, f32[1,4096]{1,0:T(1,128)S(1)}, u32[]{:S(2)}, u32[]{:S(2)}) collective-permute-start(f32[1,4096]{1,0:T(1,128)S(1)} %get-tuple-element.37), channel_id=1, source_target_pairs={{1,0},{2,1},{3,2},{4,3},{5,4},{6,5},{7,6},{0,7},{9,8},{10,9},{11,1... | collective-permute-start | bytes 49160 | tf_op jit(solution)/shard_map/ppermute | solution.py:17
  46.8 5.0 %collective-permute-start.4 = (f32[1,4096]{1,0:T(1,128)S(1)}, f32[1,4096]{1,0:T(1,128)S(1)}, u32[]{:S(2)}, u32[]{:S(2)}) collective-permute-start(f32[1,4096]{1,0:T(1,128)S(1)} %get-tuple-element.30), channel_id=1, source_target_pairs={{0,1},{1,2},{2,3},{3,4},{4,5},{5,6},{6,7},{7,0},{8,9},{9,10},{10,1... | collective-permute-start | bytes 49160 | tf_op jit(solution)/shard_map/ppermute | solution.py:16
  46.9 5.2 %collective-permute-start.5 = (f32[1,4096]{1,0:T(1,128)S(1)}, f32[1,4096]{1,0:T(1,128)S(1)}, u32[]{:S(2)}, u32[]{:S(2)}) collective-permute-start(f32[1,4096]{1,0:T(1,128)S(1)} %get-tuple-element.31), channel_id=1, source_target_pairs={{1,0},{2,1},{3,2},{4,3},{5,4},{6,5},{7,6},{0,7},{9,8},{10,9},{11,1... | collective-permute-start | bytes 49160 | tf_op jit(solution)/shard_map/ppermute | solution.py:17
  60.9 5.0 %collective-permute-start.6 = (f32[1,4096]{1,0:T(1,128)S(1)}, f32[1,4096]{1,0:T(1,128)S(1)}, u32[]{:S(2)}, u32[]{:S(2)}) collective-permute-start(f32[1,4096]{1,0:T(1,128)S(1)} %get-tuple-element.24), channel_id=1, source_target_pairs={{0,1},{1,2},{2,3},{3,4},{4,5},{5,6},{6,7},{7,0},{8,9},{9,10},{10,1... | collective-permute-start | bytes 49160 | tf_op jit(solution)/shard_map/ppermute | solution.py:16
  61.0 5.0 %collective-permute-start.7 = (f32[1,4096]{1,0:T(1,128)S(1)}, f32[1,4096]{1,0:T(1,128)S(1)}, u32[]{:S(2)}, u32[]{:S(2)}) collective-permute-start(f32[1,4096]{1,0:T(1,128)S(1)} %get-tuple-element.25), channel_id=1, source_target_pairs={{1,0},{2,1},{3,2},{4,3},{5,4},{6,5},{7,6},{0,7},{9,8},{10,9},{11,1... | collective-permute-start | bytes 49160 | tf_op jit(solution)/shard_map/ppermute | solution.py:17
  73.2 10.2 %copy-start = (f32[256,4096]{1,0:T(8,128)}, f32[256,4096]{1,0:T(8,128)S(1)}, u32[]{:S(2)}) copy-start(f32[256,4096]{1,0:T(8,128)S(1)} %fusion.7) | copy-start | bytes 12582916
  73.3 10.2 %collective-permute-start.8 = (f32[1,4096]{1,0:T(1,128)S(1)}, f32[1,4096]{1,0:T(1,128)S(1)}, u32[]{:S(2)}, u32[]{:S(2)}) collective-permute-start(f32[1,4096]{1,0:T(1,128)S(1)} %slice.321), channel_id=1, source_target_pairs={{1,0},{2,1},{3,2},{4,3},{5,4},{6,5},{7,6},{0,7},{9,8},{10,9},{11,1... | collective-permute-start | bytes 49160 | tf_op jit(solution)/shard_map/ppermute | solution.py:17
  80.4 103.1 %collective-permute-start.10 = (f32[128,4096]{1,0:T(8,128)}, f32[128,4096]{1,0:T(8,128)S(1)}, u32[]{:S(2)}, u32[]{:S(2)}) collective-permute-start(f32[128,4096]{1,0:T(8,128)} %get-tuple-element.18), channel_id=1, source_target_pairs={{0,8},{8,16},{16,24},{24,0},{1,9},{9,17},{17,25},{25,1},{2,10},{10... | collective-permute-start | bytes 6291464 | tf_op jit(solution)/shard_map/ppermute | solution.py:24
  82.4 101.1 %collective-permute-start.9 = (f32[128,4096]{1,0:T(8,128)}, f32[128,4096]{1,0:T(8,128)}, u32[]{:S(2)}, u32[]{:S(2)}) collective-permute-start(f32[128,4096]{1,0:T(8,128)} %get-tuple-element.19), channel_id=1, source_target_pairs={{0,24},{8,0},{16,8},{24,16},{1,25},{9,1},{17,9},{25,17},{2,26},{10... | collective-permute-start | bytes 6291464 | tf_op jit(solution)/shard_map/ppermute | solution.py:24
  186.9 3.6 %collective-permute-start.11 = (f32[128]{0:T(128)S(1)}, f32[128]{0:T(128)S(1)}, u32[]{:S(2)}, u32[]{:S(2)}) collective-permute-start(f32[128]{0:T(128)S(1)} %broadcast_multiply_fusion), channel_id=1, source_target_pairs={{0,24},{8,0},{16,8},{24,16},{1,25},{9,1},{17,9},{25,17},{2,26},{10... | collective-permute-start | bytes 1544 | tf_op jit(solution)/shard_map/ppermute | solution.py:24
where the time goes:
time: 191 us
  blocking collectives  86.6 us (45%)
  other arithmetic  44.8 us (23%)
  local copies, waits for them, and re-layouts  25 us (13%)
  starting transfers between devices  23.7 us (12%)
  waiting for transfers between devices  6.19 us (3%)
  between operations  4.78 us (3%)
    unnamed x1, blocking collectives  72.4 us
    select_n x4, other arithmetic, body(): lattice = jnp.where(parity == colour, fresh, lattice)  33 us
    ppermute x5, starting transfers between devices, padded_2(): after = lax.ppermute(leading, axis, down)  18.5 us
    psum x1, blocking collectives, body(): total = lax.psum(jnp.sum(row_energy), 'tile')  14.2 us
    slice x8, local copies, waits for them, and re-layouts, body(): jnp.roll(lattice, -1, 1)  14.1 us
    ppermute x3, starting transfers between devices, shifted(): lax.ppermute(value, axis, [(i, (i + by) % peers) for i in range(peers)])  4.48 us
  transfers between devices with their start and end apart: 12, of which 6 were waited for; matrix products, arithmetic and copies ran while one was open for 14% of the time, Pallas kernels for 0%

commit v1 on v0

v1 whole, which is shorter than its diff:
```python
import functools

import jax
import jax.numpy as jnp
from jax import lax
from jax.experimental import pallas as pl
from jax.experimental.pallas import tpu as pltpu
from jax.sharding import PartitionSpec as P

SWEEPS = 2
H = 16
LANES = 128
STAGES = 2 * SWEEPS
MESH = pl.DeviceIdType.MESH


def fold_lanes(value):
    total = value[:, :LANES]
    for k in range(1, value.shape[1] // LANES):
        total = total + value[:, k * LANES : (k + 1) * LANES]
    return total


def with_sides(ref, t, start, width, cols):
    before = (start - LANES) % cols
    after = (start + width) % cols
    return jnp.concatenate(
        [
            ref[t, :, before : before + LANES],
            ref[t, :, start : start + width],
            ref[t, :, after : after + LANES],
        ],
        axis=1,
    )


def kernel(
    n, peers, total_rows,
    spins_ref, noise_ref, betas_ref, labels_ref, accept_ref,
    out_ref, energy_ref, margin_ref, label_out, log_out, beta_out,
    S, N, R, NH, NR, EP, MP, MR, EM, EG, LM, LG,
    s_sem, n_sem, o_sem, hs_sem, hr_sem, bs_sem, br_sem,
    ms_sem, mr_sem, es_sem, er_sem, ls_sem, lr_sem,
):
    _, rows, cols = spins_ref.shape
    T = rows // H
    width = min(1024, cols)
    me = lax.axis_index("rep")
    tile = lax.axis_index("tile")
    nxt = lax.rem(tile + 1, peers)
    prv = lax.rem(tile + peers - 1, peers)

    def load_spins(t):
        return pltpu.make_async_copy(spins_ref.at[0, pl.ds(pl.multiple_of(t * H, H), H)], S.at[t + 1], s_sem.at[t])

    def load_noise(w, t):
        return pltpu.make_async_copy(
            noise_ref.at[w, 0, pl.ds(pl.multiple_of(t * H, H), H)], N.at[w, t + 1], n_sem.at[w, t]
        )

    def load(t):
        load_spins(t).start()
        for w in range(SWEEPS):
            load_noise(w, t).start()

    def loaded(t):
        load_spins(t).wait()
        for w in range(SWEEPS):
            load_noise(w, t).wait()

    barrier = pltpu.get_barrier_semaphore()

    @pl.loop(1, peers)
    def _(d):
        pl.semaphore_signal(barrier, inc=1, device_id={"tile": lax.rem(tile + d, peers)}, device_id_type=MESH)

    @pl.loop(1, n)
    def _(d):
        pl.semaphore_signal(barrier, inc=1, device_id={"rep": lax.rem(me + d, n)}, device_id_type=MESH)

    load(0)
    load(T - 1)

    @pl.loop(1, T - 1)
    def _(t):
        load(t)

    beta = jnp.float32(0.0)
    for k in range(n):
        beta = beta + jnp.where(labels_ref[0] == k, betas_ref[k], 0.0)

    loaded(0)
    loaded(T - 1)
    for w in range(SWEEPS):
        NH[0, w] = N[w, T].astype(jnp.float32)
        NH[1, w] = N[w, 1].astype(jnp.float32)

    pl.semaphore_wait(barrier, n - 1 + peers - 1)

    def halo_copies():
        copies = []
        for side, (start, slot, dev) in enumerate(((rows - H, 0, nxt), (0, T + 1, prv))):
            copies.append(
                pltpu.make_async_remote_copy(
                    spins_ref.at[0, pl.ds(start, H)], S.at[slot], hs_sem.at[side, 0], hr_sem.at[side, 0],
                    device_id={"tile": dev}, device_id_type=MESH,
                )
            )
            for w in range(SWEEPS):
                copies.append(
                    pltpu.make_async_remote_copy(
                        NH.at[side, w], NR.at[side, w], hs_sem.at[side, 1 + w], hr_sem.at[side, 1 + w],
                        device_id={"tile": dev}, device_id_type=MESH,
                    )
                )
        return copies

    halos = halo_copies()
    for copy in halos:
        copy.start()

    def bulk(t):
        dest = lax.rem(t, n)
        q = t // n
        return pltpu.make_async_remote_copy(
            S.at[t + 1], R.at[me, q], bs_sem.at[t], br_sem.at[me, q],
            device_id={"rep": dest}, device_id_type=MESH,
        )

    def store_out(t):
        return pltpu.make_async_copy(S.at[t + 1], out_ref.at[0, pl.ds(pl.multiple_of(t * H, H), H)], o_sem.at[t])

    row = lax.broadcasted_iota(jnp.int32, (H, width), 0)
    parity = (row + lax.broadcasted_iota(jnp.int32, (H, width), 1)) % 2

    def update(t, stage):
        sweep, colour = stage // 2, stage % 2
        i = t + 1
        above = jnp.maximum(i - 1, 0)
        below = jnp.minimum(i + 1, T + 1)
        for b in range(cols // width):
            c0 = b * width
            cs = slice(c0, c0 + width)
            ext = with_sides(S, i, c0, width, cols)
            cur = ext[:, LANES : LANES + width]
            left = pltpu.roll(ext, 1, 1)[:, LANES : LANES + width]
            right = pltpu.roll(ext, width + 2 * LANES - 1, 1)[:, LANES : LANES + width]
            up = jnp.where(row == 0, S[above, H - 1 : H, cs], pltpu.roll(cur, 1, 0))
            down = jnp.where(row == H - 1, S[below, 0:1, cs], pltpu.roll(cur, H - 1, 0))
            field = (up + down) + (left + right)
            fresh = jnp.tanh(beta * field + N[sweep, i, :, cs].astype(jnp.float32))
            S[i, :, cs] = jnp.where(parity == colour, fresh, cur)

    def finish(t):
        i = t + 1

        @pl.when(lax.rem(t, n) != me)
        def _():
            bulk(t).start()

        store_out(t).start()
        total = jnp.zeros((H, LANES), jnp.float32)
        for b in range(cols // width):
            c0 = b * width
            cs = slice(c0, c0 + width)
            cur = S[i, :, cs]
            after = (c0 + width) % cols
            ext = jnp.concatenate([cur, S[i, :, after : after + LANES]], axis=1)
            right = pltpu.roll(ext, width + LANES - 1, 1)[:, :width]
            down = jnp.where(row == H - 1, S[i + 1, 0:1, cs], pltpu.roll(cur, H - 1, 0))
            total = total + fold_lanes(cur * (down + right))
        EP[t] = total

    loaded(1)

    @pl.loop(1, T + STAGES)
    def _(s):
        @pl.when(s + 1 < T - 1)
        def _():
            loaded(s + 1)

        @pl.when(s == T - 1)
        def _():
            for copy in halos[1 + SWEEPS :]:
                copy.wait_recv()
            for w in range(SWEEPS):
                N[w, T + 1] = NR[1, w].astype(jnp.bfloat16)

        for k in range(STAGES):
            t = s - k

            @pl.when((t >= k + 1) & (t <= T))
            def _():
                update(t, k)

        @pl.when(s - STAGES >= STAGES)
        def _():
            finish(s - STAGES)

    for copy in halos[: 1 + SWEEPS]:
        copy.wait_recv()
    for w in range(SWEEPS):
        N[w, 0] = NR[0, w].astype(jnp.bfloat16)

    for k in range(STAGES):

        @pl.loop(-1 if k < STAGES - 1 else 0, k + 1)
        def _(t):
            update(t, k)

    @pl.loop(0, STAGES)
    def _(t):
        finish(t)

    per_row = jnp.sum(EP[...].reshape(rows, LANES).T, axis=0, keepdims=True) * (-1.0 / cols)
    energy_ref[...] = per_row
    local = jnp.broadcast_to(jnp.sum(per_row, axis=1, keepdims=True), (8, LANES))
    EM[...] = local
    EG[tile] = local

    def energy_copy(d):
        return pltpu.make_async_remote_copy(
            EM, EG.at[tile], es_sem.at[d], er_sem.at[tile],
            device_id={"tile": lax.rem(tile + d, peers)}, device_id_type=MESH,
        )

    def energy_from(d):
        src = lax.rem(tile + d, peers)
        return pltpu.make_async_remote_copy(
            EM, EG.at[src], es_sem.at[d], er_sem.at[src], device_id={"tile": src}, device_id_type=MESH
        )

    @pl.loop(1, peers)
    def _(d):
        energy_copy(d).start()

    @pl.loop(1, peers)
    def _(d):
        energy_from(d).wait_recv()

    energy = jnp.sum(EG[...], axis=0) / total_rows
    line = lax.broadcasted_iota(jnp.int32, (8, LANES), 0)
    label_float = labels_ref[0].astype(jnp.float32)
    accept_zero = accept_ref[0, 0].astype(jnp.float32)
    accept_one = accept_ref[1, 0].astype(jnp.float32)
    message = jnp.where(
        line == 0, energy,
        jnp.where(line == 1, label_float, jnp.where(line == 2, accept_zero, accept_one)),
    )
    LM[...] = message
    LG[me] = message

    def ladder_copy(d):
        return pltpu.make_async_remote_copy(
            LM, LG.at[me], ls_sem.at[d], lr_sem.at[me],
            device_id={"rep": lax.rem(me + d, n)}, device_id_type=MESH,
        )

    def ladder_from(d):
        src = lax.rem(me + d, n)
        return pltpu.make_async_remote_copy(
            LM, LG.at[src], ls_sem.at[d], lr_sem.at[src], device_id={"rep": src}, device_id_type=MESH
        )

    @pl.loop(1, n)
    def _(d):
        ladder_copy(d).start()

    def margin_copy(q, d):
        dest = lax.rem(me + d, n)
        return pltpu.make_async_remote_copy(
            MP.at[dest, q], MR.at[q * n + me], ms_sem.at[q, d], mr_sem.at[q * n + me],
            device_id={"rep": dest}, device_id_type=MESH,
        )

    def margin_from(t):
        src = lax.rem(t, n)
        return pltpu.make_async_remote_copy(
            MP.at[0, 0], MR.at[t], ms_sem.at[0, 1], mr_sem.at[t], device_id={"rep": src}, device_id_type=MESH
        )

    def bulk_from(src, q):
        return pltpu.make_async_remote_copy(
            S.at[1], R.at[src, q], bs_sem.at[0], br_sem.at[src, q], device_id={"rep": src}, device_id_type=MESH
        )

    @pl.loop(0, T // n)
    def _(q):
        R[me, q] = S[q * n + me + 1]

        @pl.loop(1, n)
        def _(d):
            bulk_from(lax.rem(me + d, n), q).wait_recv()

        totals = [jnp.zeros((H, LANES), jnp.float32) for _ in range(n)]
        chunk = min(512, cols)
        for b in range(cols // chunk):
            cs = slice(b * chunk, (b + 1) * chunk)
            parts = [R[r, q, :, cs] for r in range(n)]
            for r in range(n):
                totals[r] = totals[r] + fold_lanes(parts[r] * parts[(r + 1) % n])
        for r in range(n):
            MP[r, q] = totals[r]
        MR[q * n + me] = MP[me, q]

        @pl.loop(1, n)
        def _(d):
            margin_copy(q, d).start()

    @pl.loop(1, n)
    def _(d):
        ladder_from(d).wait_recv()

    energies = [LG[r][0:1] for r in range(n)]
    labels = [LG[r][1:2] for r in range(n)]
    acc = [[LG[r][2 + p : 3 + p] for r in range(n)] for p in range(2)]

    def beta_of(label):
        value = jnp.zeros((1, LANES), jnp.float32)
        for k in range(n):
            value = value + jnp.where(label == float(k), betas_ref[k], 0.0)
        return value

    def swapped(current, accepts, first):
        result = list(current)
        for r in range(first, n, 2):
            o = (r + 1) % n
            take = accepts[r] == 1.0
            result[r] = jnp.where(take, current[o], current[r])
            result[o] = jnp.where(take, current[r], current[o])
        return result

    labels_one = swapped(labels, acc[0], 0)
    labels_two = swapped(labels_one, acc[1], 1)
    zero = [beta_of(x) for x in labels]
    one = [beta_of(x) for x in labels_one]
    two = [beta_of(x) for x in labels_two]
    my_label = jnp.zeros((1, LANES), jnp.float32)
    my_log = my_label
    my_beta = my_label
    for r in range(n):
        o = (r + 1) % n
        betas_here = zero if r % 2 == 0 else one
        log = (betas_here[r] - betas_here[o]) * (energies[r] - energies[o])
        my_label = jnp.where(me == r, labels_two[r], my_label)
        my_log = jnp.where(me == r, log, my_log)
        my_beta = jnp.where(me == r, two[r], my_beta)
    label_out[0] = jnp.max(my_label).astype(jnp.int32)
    log_out[0] = jnp.max(my_log)
    beta_out[0] = jnp.max(my_beta)

    for copy in halos:
        copy.wait_send()

    @pl.loop(0, T)
    def _(t):
        store_out(t).wait()

        @pl.when(lax.rem(t, n) != me)
        def _():
            bulk(t).wait_send()

    @pl.loop(1, peers)
    def _(d):
        energy_copy(d).wait_send()

    @pl.loop(1, n)
    def _(d):
        ladder_copy(d).wait_send()

    @pl.loop(0, T)
    def _(t):
        @pl.when(lax.rem(t, n) != me)
        def _():
            margin_from(t).wait_recv()

    @pl.loop(0, T // n)
    def _(q):
        @pl.loop(1, n)
        def _(d):
            margin_copy(q, d).wait_send()

    margin_ref[...] = jnp.sum(MR[...].reshape(rows, LANES).T, axis=0, keepdims=True) * (1.0 / cols)


def body(n, peers, total_rows, spins_in, noise, betas, labels, accept):
    _, rows, cols = spins_in.shape
    T = rows // H
    f32 = jnp.float32
    hbm = pl.BlockSpec(memory_space=pltpu.HBM)
    smem = pl.BlockSpec(memory_space=pltpu.SMEM)
    vmem = pl.BlockSpec(memory_space=pltpu.VMEM)
    dma = pltpu.SemaphoreType.DMA
    outs = pl.pallas_call(
        functools.partial(kernel, n, peers, total_rows),
        out_shape=(
            jax.ShapeDtypeStruct(spins_in.shape, f32),
            jax.ShapeDtypeStruct((1, rows), f32),
            jax.ShapeDtypeStruct((1, rows), f32),
            jax.ShapeDtypeStruct((1,), jnp.int32),
            jax.ShapeDtypeStruct((1,), f32),
            jax.ShapeDtypeStruct((1,), f32),
        ),
        in_specs=[hbm, hbm, smem, smem, smem],
        out_specs=(hbm, vmem, vmem, smem, smem, smem),
        scratch_shapes=[
            pltpu.VMEM((T + 2, H, cols), f32),
            pltpu.VMEM((SWEEPS, T + 2, H, cols), jnp.bfloat16),
            pltpu.VMEM((n, T // n, H, cols), f32),
            pltpu.VMEM((2, SWEEPS, H, cols), f32),
            pltpu.VMEM((2, SWEEPS, H, cols), f32),
            pltpu.VMEM((T, H, LANES), f32),
            pltpu.VMEM((n, T // n, H, LANES), f32),
            pltpu.VMEM((T, H, LANES), f32),
            pltpu.VMEM((8, LANES), f32),
            pltpu.VMEM((peers, 8, LANES), f32),
            pltpu.VMEM((8, LANES), f32),
            pltpu.VMEM((n, 8, LANES), f32),
            dma((T,)),
            dma((SWEEPS, T)),
            dma((T,)),
            dma((2, 1 + SWEEPS)),
            dma((2, 1 + SWEEPS)),
            dma((T,)),
            dma((n, T // n)),
            dma((T // n, n)),
            dma((T,)),
            dma((peers,)),
            dma((peers,)),
            dma((n,)),
            dma((n,)),
        ],
        compiler_params=pltpu.CompilerParams(collective_id=0, has_side_effects=True),
        name="lattice_exchange",
    )(spins_in, noise, betas, labels, accept)
    return outs


def solution(mesh):
    n = mesh.shape["rep"]
    peers = mesh.shape["tile"]
    in_specs = (P("rep", "tile", None), P(None, "rep", "tile", None), P(), P("rep"), P(None, "rep"))
    out_specs = (P("rep", "tile", None), P("rep", "tile"), P("rep", "tile"), P("rep"), P("rep"), P("rep"))

    def run(spins_in, noise, betas, labels, accept):
        total_rows = spins_in.shape[1]
        step = jax.shard_map(
            functools.partial(body, n, peers, total_rows),
            mesh=mesh, in_specs=in_specs, out_specs=out_specs, check_vma=False,
        )
        return step(spins_in, noise, betas, labels, accept)

    return run
```

time: 191 us -> 84 us (0.44)
  blocking collectives: 86.6 us -> 0 us
  Pallas kernels: 0 us -> 70.1 us
  other arithmetic: 44.8 us -> 0 us
  starting transfers between devices: 23.7 us -> 0 us
  local copies, waits for them, and re-layouts: 25 us -> 7.08 us
  waiting for transfers between devices: 6.19 us -> 0 us
    unnamed x1 -> x0, blocking collectives: 72.4 us -> none
    pallas_call x0 -> x1, Pallas kernels: none -> 70.1 us  [body(): pl.pallas_call(functools.partial(kernel, n, peers, total_rows), out_shape...]
    select_n x7 -> x0, other arithmetic: 37.2 us -> none  [the longest x4 33 us: body(): lattice = jnp.where(parity == colour, fresh, lattice)]
    ppermute x12 -> x0, starting transfers between devices: 23.7 us -> none  [the longest x5 18.5 us: padded_2(): after = lax.ppermute(leading, axis, down)]
    slice x27 -> x0, local copies, waits for them, and re-layouts: 21.8 us -> none  [the longest x8 14.1 us: body(): jnp.roll(lattice, -1, 1)]
    psum x1 -> x0, blocking collectives: 14.2 us -> none  [body(): total = lax.psum(jnp.sum(row_energy), 'tile')]
    ppermute x12 -> x0, waiting for transfers between devices: 6.19 us -> none  [the longest x4 3.7 us: padded_2(): before = lax.ppermute(last, axis, up)]
    reduce_sum x5 -> x0, other arithmetic: 6.13 us -> none  [the longest x1 3.32 us: body(): margin_upper = jnp.mean(lattice[:half] * upper, axis=1)]
  transfers between devices with their start and end apart: 12 -> 0, of which waited for: 6 -> 0; matrix products, arithmetic and copies ran while one was open for 14% -> 0% of each run, Pallas kernels for 0% -> 0%
where the time goes in v1:
time: 84 us; the launch traced here: 83.8 us
  Pallas kernels  70.1 us (83%)
  local copies, waits for them, and re-layouts  7.08 us (8%)
  between operations  6.59 us (8%)
    pallas_call x1, Pallas kernels, body(): pl.pallas_call(functools.partial(kernel, n, peers, total_rows), out_shape...  70.1 us
    unnamed x8, local copies, waits for them, and re-layouts  7.08 us

profile of v1, /device:TPU:0, one launch (start us, length us, event | category | flops | bytes accessed | tf_op | source)
XLA Modules:
  0.0 83.8 jit_solution(15353275170835277666)
XLA Ops:
  1.3 1.3 %copy.11.accept_ref = s32[2,1]{1,0:T(2,128)} copy(s32[2,1]{0,1:T(1,128)} %param.9) | data formatting | bytes 16 | tf_op args[4]
  2.6 70.1 %lattice_exchange.1 = (f32[1,256,4096]{2,1,0:T(8,128)}, f32[1,256]{1,0:T(1,128)}, f32[1,256]{1,0:T(1,128)}, s32[1]{0:T(128)}, f32[1]{0:T(128)}, /*index=5*/f32[1]{0:T(128)}) custom-call(f32[1,256,4096]{2,1,0:T(8,128)} %spins_ref.1, bf16[2,1,256,4096]{3,2,1,0:T(8,128)(2,1)} %noise_ref.1, f32[4]{0:T(128)} %betas_ref.1, s32[1]{0:T(128)S(6)} %copy.18.labels_ref, ...), custom_call_target="tpu_custom_call" | custom-call | tf_op jit(solution)/shard_map/lattice_exchange/pallas_call | solution.py:394
  72.7 0.0 copy-start.1
  72.7 0.0 copy-start
  72.7 4.7 %copy.19 = f32[1,256,4096]{2,1,0:T(8,128)} copy(f32[1,256,4096]{2,1,0:T(8,128)} %get-tuple-element.12) | data formatting | bytes 8388608
  77.4 0.0 copy-done.1
  77.4 0.6 copy.20
  77.9 0.0 copy-done
  77.9 0.6 copy.21
Async XLA Ops:
  72.7 4.7 %copy-start.1 = (f32[1,256]{1,0:T(1,128)S(1)}, f32[1,256]{1,0:T(1,128)}, u32[]{:S(2)}) copy-start(f32[1,256]{1,0:T(1,128)} %get-tuple-element.13) | copy-start | bytes 3076
  72.7 5.2 %copy-start = (f32[1,256]{1,0:T(1,128)S(1)}, f32[1,256]{1,0:T(1,128)}, u32[]{:S(2)}) copy-start(f32[1,256]{1,0:T(1,128)} %get-tuple-element.14) | copy-start | bytes 3076

commit v2 on v1

--- a/solution.py
+++ b/solution.py
@@ -9,6 +9,7 @@
 
 SWEEPS = 2
 H = 16
+HALO = 8
 LANES = 128
 STAGES = 2 * SWEEPS
 MESH = pl.DeviceIdType.MESH
@@ -36,15 +37,16 @@
 
 def kernel(
     n, peers, total_rows,
-    spins_ref, noise_ref, betas_ref, labels_ref, accept_ref,
+    spins_ref, noise_ref, betas_hbm, labels_ref, accept_hbm,
     out_ref, energy_ref, margin_ref, label_out, log_out, beta_out,
-    S, N, R, NH, NR, EP, MP, MR, EM, EG, LM, LG,
+    S, N, R, NH, NR, EP, MP, MS, MR, EM, EG, LM, LG, betas_ref, accept_ref,
     s_sem, n_sem, o_sem, hs_sem, hr_sem, bs_sem, br_sem,
-    ms_sem, mr_sem, es_sem, er_sem, ls_sem, lr_sem,
+    ms_sem, mr_sem, es_sem, er_sem, ls_sem, lr_sem, i_sem,
 ):
     _, rows, cols = spins_ref.shape
     T = rows // H
     width = min(1024, cols)
+    share = cols // n
     me = lax.axis_index("rep")
     tile = lax.axis_index("tile")
     nxt = lax.rem(tile + 1, peers)
@@ -78,6 +80,14 @@
     def _(d):
         pl.semaphore_signal(barrier, inc=1, device_id={"rep": lax.rem(me + d, n)}, device_id_type=MESH)
 
+    small = [
+        pltpu.make_async_copy(src, dst, i_sem.at[k])
+        for k, (src, dst) in enumerate(
+            ((betas_hbm, betas_ref), (accept_hbm, accept_ref))
+        )
+    ]
+    for copy in small:
+        copy.start()
     load(0)
     load(T - 1)
 
@@ -85,6 +95,8 @@
     def _(t):
         load(t)
 
+    for copy in small:
+        copy.wait()
     beta = jnp.float32(0.0)
     for k in range(n):
         beta = beta + jnp.where(labels_ref[0] == k, betas_ref[k], 0.0)
@@ -92,17 +104,17 @@
     loaded(0)
     loaded(T - 1)
     for w in range(SWEEPS):
-        NH[0, w] = N[w, T].astype(jnp.float32)
-        NH[1, w] = N[w, 1].astype(jnp.float32)
+        NH[0, w] = N[w, T].astype(jnp.float32)[H - HALO :]
+        NH[1, w] = N[w, 1].astype(jnp.float32)[:HALO]
 
     pl.semaphore_wait(barrier, n - 1 + peers - 1)
 
     def halo_copies():
         copies = []
-        for side, (start, slot, dev) in enumerate(((rows - H, 0, nxt), (0, T + 1, prv))):
+        for side, (start, slot, dev) in enumerate(((rows - HALO, 0, nxt), (0, T + 1, prv))):
             copies.append(
                 pltpu.make_async_remote_copy(
-                    spins_ref.at[0, pl.ds(start, H)], S.at[slot], hs_sem.at[side, 0], hr_sem.at[side, 0],
+                    spins_ref.at[0, pl.ds(start, HALO)], S.at[slot, pl.ds((H - HALO) * (1 - side), HALO)], hs_sem.at[side, 0], hr_sem.at[side, 0],
                     device_id={"tile": dev}, device_id_type=MESH,
                 )
             )
@@ -119,11 +131,13 @@
     for copy in halos:
         copy.start()
 
-    def bulk(t):
-        dest = lax.rem(t, n)
-        q = t // n
-        return pltpu.make_async_remote_copy(
-            S.at[t + 1], R.at[me, q], bs_sem.at[t], br_sem.at[me, q],
+    def share_of(d):
+        return pl.ds(pl.multiple_of(d * share, LANES), share)
+
+    def bulk(t, d):
+        dest = lax.rem(me + d, n)
+        return pltpu.make_async_remote_copy(
+            S.at[t + 1, :, share_of(dest)], R.at[me, t], bs_sem.at[t, d], br_sem.at[me, t],
             device_id={"rep": dest}, device_id_type=MESH,
         )
 
@@ -154,11 +168,10 @@
     def finish(t):
         i = t + 1
 
-        @pl.when(lax.rem(t, n) != me)
-        def _():
-            bulk(t).start()
-
+        for d in range(1, n):
+            bulk(t, d).start()
         store_out(t).start()
+        R[me, t] = S[i, :, share_of(me)]
         total = jnp.zeros((H, LANES), jnp.float32)
         for b in range(cols // width):
             c0 = b * width
@@ -184,7 +197,7 @@
             for copy in halos[1 + SWEEPS :]:
                 copy.wait_recv()
             for w in range(SWEEPS):
-                N[w, T + 1] = NR[1, w].astype(jnp.bfloat16)
+                N[w, T + 1] = jnp.concatenate([NR[1, w], NR[1, w]], axis=0).astype(jnp.bfloat16)
 
         for k in range(STAGES):
             t = s - k
@@ -200,7 +213,7 @@
     for copy in halos[: 1 + SWEEPS]:
         copy.wait_recv()
     for w in range(SWEEPS):
-        N[w, 0] = NR[0, w].astype(jnp.bfloat16)
+        N[w, 0] = jnp.concatenate([NR[0, w], NR[0, w]], axis=0).astype(jnp.bfloat16)
 
     for k in range(STAGES):
 
@@ -242,7 +255,7 @@
     line = lax.broadcasted_iota(jnp.int32, (8, LANES), 0)
     label_float = labels_ref[0].astype(jnp.float32)
     accept_zero = accept_ref[0, 0].astype(jnp.float32)
-    accept_one = accept_ref[1, 0].astype(jnp.float32)
+    accept_one = accept_ref[0, 1].astype(jnp.float32)
     message = jnp.where(
         line == 0, energy,
         jnp.where(line == 1, label_float, jnp.where(line == 2, accept_zero, accept_one)),
@@ -266,46 +279,46 @@
     def _(d):
         ladder_copy(d).start()
 
-    def margin_copy(q, d):
+    def bulk_from(d, t):
+        src = lax.rem(me + d, n)
+        return pltpu.make_async_remote_copy(
+            S.at[1, :, share_of(0)], R.at[src, t], bs_sem.at[0, 1], br_sem.at[src, t],
+            device_id={"rep": src}, device_id_type=MESH,
+        )
+
+    @pl.loop(STAGES, T + STAGES)
+    def _(s):
+        t = lax.rem(s, T)
+        for d in range(1, n):
+            bulk_from(d, t).wait_recv()
+        totals = [jnp.zeros((H, LANES), jnp.float32) for _ in range(n)]
+        for b in range(share // LANES):
+            cs = slice(b * LANES, (b + 1) * LANES)
+            parts = [R[r, t, :, cs] for r in range(n)]
+            for r in range(n):
+                totals[r] = totals[r] + parts[r] * parts[(r + 1) % n]
+        for r in range(n):
+            MP[r, t] = totals[r]
+
+    for r in range(n):
+        sums = jnp.sum(MP[r].reshape(rows, LANES).T, axis=0, keepdims=True)
+        MS[r] = jnp.broadcast_to(sums, (8, rows))
+    MR[me] = MS[me]
+
+    def margin_copy(d):
         dest = lax.rem(me + d, n)
         return pltpu.make_async_remote_copy(
-            MP.at[dest, q], MR.at[q * n + me], ms_sem.at[q, d], mr_sem.at[q * n + me],
-            device_id={"rep": dest}, device_id_type=MESH,
-        )
-
-    def margin_from(t):
-        src = lax.rem(t, n)
-        return pltpu.make_async_remote_copy(
-            MP.at[0, 0], MR.at[t], ms_sem.at[0, 1], mr_sem.at[t], device_id={"rep": src}, device_id_type=MESH
-        )
-
-    def bulk_from(src, q):
-        return pltpu.make_async_remote_copy(
-            S.at[1], R.at[src, q], bs_sem.at[0], br_sem.at[src, q], device_id={"rep": src}, device_id_type=MESH
-        )
-
-    @pl.loop(0, T // n)
-    def _(q):
-        R[me, q] = S[q * n + me + 1]
-
-        @pl.loop(1, n)
-        def _(d):
-            bulk_from(lax.rem(me + d, n), q).wait_recv()
-
-        totals = [jnp.zeros((H, LANES), jnp.float32) for _ in range(n)]
-        chunk = min(512, cols)
-        for b in range(cols // chunk):
-            cs = slice(b * chunk, (b + 1) * chunk)
-            parts = [R[r, q, :, cs] for r in range(n)]
-            for r in range(n):
-                totals[r] = totals[r] + fold_lanes(parts[r] * parts[(r + 1) % n])
-        for r in range(n):
-            MP[r, q] = totals[r]
-        MR[q * n + me] = MP[me, q]
-
-        @pl.loop(1, n)
-        def _(d):
-            margin_copy(q, d).start()
+            MS.at[dest], MR.at[me], ms_sem.at[d], mr_sem.at[me], device_id={"rep": dest}, device_id_type=MESH
+        )
+
+    def margin_from(d):
+        src = lax.rem(me + d, n)
+        return pltpu.make_async_remote_copy(
+            MS.at[0], MR.at[src], ms_sem.at[d], mr_sem.at[src], device_id={"rep": src}, device_id_type=MESH
+        )
+
+    for d in range(1, n):
+        margin_copy(d).start()
 
     @pl.loop(1, n)
     def _(d):
@@ -355,32 +368,48 @@
     @pl.loop(0, T)
     def _(t):
         store_out(t).wait()
-
-        @pl.when(lax.rem(t, n) != me)
-        def _():
-            bulk(t).wait_send()
+        for d in range(1, n):
+            bulk(t, d).wait_send()
 
     @pl.loop(1, peers)
     def _(d):
         energy_copy(d).wait_send()
 
-    @pl.loop(1, n)
-    def _(d):
+    for d in range(1, n):
         ladder_copy(d).wait_send()
-
-    @pl.loop(0, T)
-    def _(t):
-        @pl.when(lax.rem(t, n) != me)
-        def _():
-            margin_from(t).wait_recv()
-
-    @pl.loop(0, T // n)
-    def _(q):
-        @pl.loop(1, n)
-        def _(d):
-            margin_copy(q, d).wait_send()
-
-    margin_ref[...] = jnp.sum(MR[...].reshape(rows, LANES).T, axis=0, keepdims=True) * (1.0 / cols)
+        margin_from(d).wait_recv()
+        margin_copy(d).wait_send()
+
+    margin_ref[...] = jnp.sum(MR[...], axis=0)[0:1] * (1.0 / cols)
+
+
+def settle(spins, *refs):
+    count = (len(refs) - 4) // 2
+    sources, outs = refs[:count], refs[count + 1 : 2 * count + 1]
+    out = refs[count]
+    buffer, in_sem, out_sem, small_sem = refs[2 * count + 1 :]
+    pieces = buffer.shape[0]
+    height = buffer.shape[1]
+
+    def copies(k):
+        place = pl.ds(k * height, height)
+        return (
+            pltpu.make_async_copy(spins.at[0, place], buffer.at[k], in_sem.at[k]),
+            pltpu.make_async_copy(buffer.at[k], out.at[0, place], out_sem.at[k]),
+        )
+
+    small = [pltpu.make_async_copy(a, b, small_sem.at[k]) for k, (a, b) in enumerate(zip(sources, outs))]
+    for k in range(pieces):
+        copies(k)[0].start()
+    for copy in small:
+        copy.start()
+    for k in range(pieces):
+        copies(k)[0].wait()
+        copies(k)[1].start()
+    for k in range(pieces):
+        copies(k)[1].wait()
+    for copy in small:
+        copy.wait()
 
 
 def body(n, peers, total_rows, spins_in, noise, betas, labels, accept):
@@ -391,7 +420,8 @@
     smem = pl.BlockSpec(memory_space=pltpu.SMEM)
     vmem = pl.BlockSpec(memory_space=pltpu.VMEM)
     dma = pltpu.SemaphoreType.DMA
-    outs = pl.pallas_call(
+    accept = jnp.transpose(accept)
+    results = pl.pallas_call(
         functools.partial(kernel, n, peers, total_rows),
         out_shape=(
             jax.ShapeDtypeStruct(spins_in.shape, f32),
@@ -401,39 +431,56 @@
             jax.ShapeDtypeStruct((1,), f32),
             jax.ShapeDtypeStruct((1,), f32),
         ),
-        in_specs=[hbm, hbm, smem, smem, smem],
+        in_specs=[hbm, hbm, hbm, smem, hbm],
         out_specs=(hbm, vmem, vmem, smem, smem, smem),
         scratch_shapes=[
             pltpu.VMEM((T + 2, H, cols), f32),
             pltpu.VMEM((SWEEPS, T + 2, H, cols), jnp.bfloat16),
-            pltpu.VMEM((n, T // n, H, cols), f32),
-            pltpu.VMEM((2, SWEEPS, H, cols), f32),
-            pltpu.VMEM((2, SWEEPS, H, cols), f32),
+            pltpu.VMEM((n, T, H, cols // n), f32),
+            pltpu.VMEM((2, SWEEPS, HALO, cols), f32),
+            pltpu.VMEM((2, SWEEPS, HALO, cols), f32),
             pltpu.VMEM((T, H, LANES), f32),
-            pltpu.VMEM((n, T // n, H, LANES), f32),
-            pltpu.VMEM((T, H, LANES), f32),
+            pltpu.VMEM((n, T, H, LANES), f32),
+            pltpu.VMEM((n, 8, rows), f32),
+            pltpu.VMEM((n, 8, rows), f32),
             pltpu.VMEM((8, LANES), f32),
             pltpu.VMEM((peers, 8, LANES), f32),
             pltpu.VMEM((8, LANES), f32),
             pltpu.VMEM((n, 8, LANES), f32),
+            pltpu.SMEM(betas.shape, f32),
+            pltpu.SMEM(accept.shape, jnp.int32),
             dma((T,)),
             dma((SWEEPS, T)),
             dma((T,)),
             dma((2, 1 + SWEEPS)),
             dma((2, 1 + SWEEPS)),
-            dma((T,)),
-            dma((n, T // n)),
-            dma((T // n, n)),
-            dma((T,)),
+            dma((T, n)),
+            dma((n, T)),
+            dma((n,)),
+            dma((n,)),
             dma((peers,)),
             dma((peers,)),
             dma((n,)),
             dma((n,)),
+            dma((2,)),
         ],
         compiler_params=pltpu.CompilerParams(collective_id=0, has_side_effects=True),
         name="lattice_exchange",
     )(spins_in, noise, betas, labels, accept)
-    return outs
+    pieces = 8
+    return pl.pallas_call(
+        settle,
+        out_shape=tuple(jax.ShapeDtypeStruct(x.shape, x.dtype) for x in results),
+        in_specs=[hbm] * len(results),
+        out_specs=(hbm,) * len(results),
+        scratch_shapes=[
+            pltpu.VMEM((pieces, rows // pieces, cols), f32),
+            dma((pieces,)),
+            dma((pieces,)),
+            dma((len(results) - 1,)),
+        ],
+        name="settle",
+    )(*results)
 
 
 def solution(mesh):

time: 84 us -> 71.7 us (0.85)
  local copies, waits for them, and re-layouts: 7.08 us -> 0 us
  between operations: 6.59 us -> 1.29 us
    unnamed x8 -> x0, local copies, waits for them, and re-layouts: 7.08 us -> none
    pallas_call x0 -> x1, Pallas kernels: none -> 5.43 us  [body(): pl.pallas_call(settle, out_shape=tuple((jax.ShapeDtypeStruct(x.shape, x.d...]
    pallas_call x1, Pallas kernels: 70.1 us -> 64.8 us  [body(): pl.pallas_call(functools.partial(kernel, n, peers, total_rows), out_shape...]
where the time goes in v2:
time: 71.7 us; the launch traced here: 71.5 us
  Pallas kernels  70.2 us (98%)
  between operations  1.29 us (2%)
    pallas_call x1, Pallas kernels, body(): pl.pallas_call(functools.partial(kernel, n, peers, total_rows), out_shape...  64.8 us
    pallas_call x1, Pallas kernels, body(): pl.pallas_call(settle, out_shape=tuple((jax.ShapeDtypeStruct(x.shape, x.d...  5.43 us

profile of v2, /device:TPU:0, one launch (start us, length us, event | category | flops | bytes accessed | tf_op | source)
XLA Modules:
  0.0 71.5 jit_solution(8399599441365404096)
XLA Ops:
  1.3 64.8 %lattice_exchange.1 = (f32[1,256,4096]{2,1,0:T(8,128)}, f32[1,256]{1,0:T(1,128)}, f32[1,256]{1,0:T(1,128)}, s32[1]{0:T(128)}, f32[1]{0:T(128)}, /*index=5*/f32[1]{0:T(128)}) custom-call(f32[1,256,4096]{2,1,0:T(8,128)} %spins_ref.1, bf16[2,1,256,4096]{3,2,1,0:T(8,128)(2,1)} %noise_ref.1, f32[4]{0:T(128)} %betas_hbm.1, s32[1]{0:T(128)S(6)} %copy.11.labels_ref, ...), custom_call_target="tpu_custom_call" | custom-call | tf_op jit(solution)/shard_map/lattice_exchange/pallas_call | solution.py:424
  66.0 5.4 %settle.1 = (f32[1,256,4096]{2,1,0:T(8,128)}, f32[1,256]{1,0:T(1,128)}, f32[1,256]{1,0:T(1,128)}, s32[1]{0:T(128)}, f32[1]{0:T(128)}, /*index=5*/f32[1]{0:T(128)}) custom-call(f32[1,256,4096]{2,1,0:T(8,128)} %get-tuple-element.12.spins, f32[1,256]{1,0:T(1,128)} %get-tuple-element.13.refs_0_, f32[1,256]{1,0:T(1,128)} %get-tuple-element.14.refs_1_, ...), custom_call_target="tpu_custom_call" | custom-call | tf_op jit(solution)/shard_map/settle/pallas_call | solution.py:471

commit v3 on v2

--- a/solution.py
+++ b/solution.py
@@ -8,9 +8,10 @@
 from jax.sharding import PartitionSpec as P
 
 SWEEPS = 2
-H = 16
-HALO = 8
+H = 8
+GROUP = 2
 LANES = 128
+VMEM_BYTES = 60 * 1024 * 1024
 STAGES = 2 * SWEEPS
 MESH = pl.DeviceIdType.MESH
 
@@ -40,7 +41,7 @@
     spins_ref, noise_ref, betas_hbm, labels_ref, accept_hbm,
     out_ref, energy_ref, margin_ref, label_out, log_out, beta_out,
     S, N, R, NH, NR, EP, MP, MS, MR, EM, EG, LM, LG, betas_ref, accept_ref,
-    s_sem, n_sem, o_sem, hs_sem, hr_sem, bs_sem, br_sem,
+    s_sem, n_sem, hs_sem, hr_sem, bs_sem, br_sem,
     ms_sem, mr_sem, es_sem, er_sem, ls_sem, lr_sem, i_sem,
 ):
     _, rows, cols = spins_ref.shape
@@ -88,10 +89,7 @@
     ]
     for copy in small:
         copy.start()
-    load(0)
-    load(T - 1)
-
-    @pl.loop(1, T - 1)
+    @pl.loop(0, T)
     def _(t):
         load(t)
 
@@ -101,20 +99,12 @@
     for k in range(n):
         beta = beta + jnp.where(labels_ref[0] == k, betas_ref[k], 0.0)
 
-    loaded(0)
-    loaded(T - 1)
-    for w in range(SWEEPS):
-        NH[0, w] = N[w, T].astype(jnp.float32)[H - HALO :]
-        NH[1, w] = N[w, 1].astype(jnp.float32)[:HALO]
-
-    pl.semaphore_wait(barrier, n - 1 + peers - 1)
-
     def halo_copies():
         copies = []
-        for side, (start, slot, dev) in enumerate(((rows - HALO, 0, nxt), (0, T + 1, prv))):
+        for side, (start, slot, dev) in enumerate(((rows - H, 0, nxt), (0, T + 1, prv))):
             copies.append(
                 pltpu.make_async_remote_copy(
-                    spins_ref.at[0, pl.ds(start, HALO)], S.at[slot, pl.ds((H - HALO) * (1 - side), HALO)], hs_sem.at[side, 0], hr_sem.at[side, 0],
+                    spins_ref.at[0, pl.ds(start, H)], S.at[slot], hs_sem.at[side, 0], hr_sem.at[side, 0],
                     device_id={"tile": dev}, device_id_type=MESH,
                 )
             )
@@ -128,21 +118,17 @@
         return copies
 
     halos = halo_copies()
-    for copy in halos:
-        copy.start()
 
     def share_of(d):
         return pl.ds(pl.multiple_of(d * share, LANES), share)
 
-    def bulk(t, d):
+    def bulk(p, d):
         dest = lax.rem(me + d, n)
         return pltpu.make_async_remote_copy(
-            S.at[t + 1, :, share_of(dest)], R.at[me, t], bs_sem.at[t, d], br_sem.at[me, t],
+            S.at[pl.ds(p * GROUP + 1, GROUP), :, share_of(dest)], R.at[me, pl.ds(p * GROUP, GROUP)],
+            bs_sem.at[p, d], br_sem.at[me, p],
             device_id={"rep": dest}, device_id_type=MESH,
         )
-
-    def store_out(t):
-        return pltpu.make_async_copy(S.at[t + 1], out_ref.at[0, pl.ds(pl.multiple_of(t * H, H), H)], o_sem.at[t])
 
     row = lax.broadcasted_iota(jnp.int32, (H, width), 0)
     parity = (row + lax.broadcasted_iota(jnp.int32, (H, width), 1)) % 2
@@ -168,15 +154,13 @@
     def finish(t):
         i = t + 1
 
-        for d in range(1, n):
-            bulk(t, d).start()
-        store_out(t).start()
         R[me, t] = S[i, :, share_of(me)]
         total = jnp.zeros((H, LANES), jnp.float32)
         for b in range(cols // width):
             c0 = b * width
             cs = slice(c0, c0 + width)
             cur = S[i, :, cs]
+            out_ref[0, pl.ds(pl.multiple_of(t * H, H), H), cs] = cur
             after = (c0 + width) % cols
             ext = jnp.concatenate([cur, S[i, :, after : after + LANES]], axis=1)
             right = pltpu.roll(ext, width + LANES - 1, 1)[:, :width]
@@ -184,20 +168,35 @@
             total = total + fold_lanes(cur * (down + right))
         EP[t] = total
 
+    def send(p):
+        for d in range(1, n):
+            bulk(p, d).start()
+
+    loaded(0)
     loaded(1)
 
     @pl.loop(1, T + STAGES)
     def _(s):
-        @pl.when(s + 1 < T - 1)
+        @pl.when((s + 1 < T) & (s < T // 2 - 1))
         def _():
             loaded(s + 1)
+
+        @pl.when(s == T // 2 - 1)
+        def _():
+            @pl.loop(T // 2, T)
+            def _(t):
+                loaded(t)
+
+        @pl.when(s == 2 * STAGES + GROUP - 1)
+        def _():
+            pl.semaphore_wait(barrier, n - 1 + peers - 1)
 
         @pl.when(s == T - 1)
         def _():
             for copy in halos[1 + SWEEPS :]:
                 copy.wait_recv()
             for w in range(SWEEPS):
-                N[w, T + 1] = jnp.concatenate([NR[1, w], NR[1, w]], axis=0).astype(jnp.bfloat16)
+                N[w, T + 1] = NR[1, w].astype(jnp.bfloat16)
 
         for k in range(STAGES):
             t = s - k
@@ -208,12 +207,25 @@
 
         @pl.when(s - STAGES >= STAGES)
         def _():
-            finish(s - STAGES)
+            t = s - STAGES
+            finish(t)
+
+            @pl.when(lax.rem(t, GROUP) == GROUP - 1)
+            def _():
+                send(t // GROUP)
+
+        @pl.when(s == T // 2)
+        def _():
+            for w in range(SWEEPS):
+                NH[0, w] = N[w, T].astype(jnp.float32)
+                NH[1, w] = N[w, 1].astype(jnp.float32)
+            for copy in halos:
+                copy.start()
 
     for copy in halos[: 1 + SWEEPS]:
         copy.wait_recv()
     for w in range(SWEEPS):
-        N[w, 0] = jnp.concatenate([NR[0, w], NR[0, w]], axis=0).astype(jnp.bfloat16)
+        N[w, 0] = NR[0, w].astype(jnp.bfloat16)
 
     for k in range(STAGES):
 
@@ -224,6 +236,10 @@
     @pl.loop(0, STAGES)
     def _(t):
         finish(t)
+
+    @pl.loop(0, STAGES // GROUP)
+    def _(p):
+        send(p)
 
     per_row = jnp.sum(EP[...].reshape(rows, LANES).T, axis=0, keepdims=True) * (-1.0 / cols)
     energy_ref[...] = per_row
@@ -279,26 +295,28 @@
     def _(d):
         ladder_copy(d).start()
 
-    def bulk_from(d, t):
+    def bulk_from(d, p):
         src = lax.rem(me + d, n)
         return pltpu.make_async_remote_copy(
-            S.at[1, :, share_of(0)], R.at[src, t], bs_sem.at[0, 1], br_sem.at[src, t],
-            device_id={"rep": src}, device_id_type=MESH,
-        )
-
-    @pl.loop(STAGES, T + STAGES)
+            S.at[pl.ds(1, GROUP), :, share_of(0)], R.at[src, pl.ds(p * GROUP, GROUP)],
+            bs_sem.at[0, 1], br_sem.at[src, p], device_id={"rep": src}, device_id_type=MESH,
+        )
+
+    @pl.loop(STAGES // GROUP, (T + STAGES) // GROUP)
     def _(s):
-        t = lax.rem(s, T)
+        p = lax.rem(s, T // GROUP)
         for d in range(1, n):
-            bulk_from(d, t).wait_recv()
-        totals = [jnp.zeros((H, LANES), jnp.float32) for _ in range(n)]
-        for b in range(share // LANES):
-            cs = slice(b * LANES, (b + 1) * LANES)
-            parts = [R[r, t, :, cs] for r in range(n)]
+            bulk_from(d, p).wait_recv()
+        for g in range(GROUP):
+            t = p * GROUP + g
+            totals = [jnp.zeros((H, LANES), jnp.float32) for _ in range(n)]
+            for b in range(share // LANES):
+                cs = slice(b * LANES, (b + 1) * LANES)
+                parts = [R[r, t, :, cs] for r in range(n)]
+                for r in range(n):
+                    totals[r] = totals[r] + parts[r] * parts[(r + 1) % n]
             for r in range(n):
-                totals[r] = totals[r] + parts[r] * parts[(r + 1) % n]
-        for r in range(n):
-            MP[r, t] = totals[r]
+                MP[r, t] = totals[r]
 
     for r in range(n):
         sums = jnp.sum(MP[r].reshape(rows, LANES).T, axis=0, keepdims=True)
@@ -365,11 +383,10 @@
     for copy in halos:
         copy.wait_send()
 
-    @pl.loop(0, T)
-    def _(t):
-        store_out(t).wait()
+    @pl.loop(0, T // GROUP)
+    def _(p):
         for d in range(1, n):
-            bulk(t, d).wait_send()
+            bulk(p, d).wait_send()
 
     @pl.loop(1, peers)
     def _(d):
@@ -384,31 +401,15 @@
 
 
 def settle(spins, *refs):
-    count = (len(refs) - 4) // 2
-    sources, outs = refs[:count], refs[count + 1 : 2 * count + 1]
-    out = refs[count]
-    buffer, in_sem, out_sem, small_sem = refs[2 * count + 1 :]
-    pieces = buffer.shape[0]
-    height = buffer.shape[1]
-
-    def copies(k):
-        place = pl.ds(k * height, height)
-        return (
-            pltpu.make_async_copy(spins.at[0, place], buffer.at[k], in_sem.at[k]),
-            pltpu.make_async_copy(buffer.at[k], out.at[0, place], out_sem.at[k]),
-        )
-
-    small = [pltpu.make_async_copy(a, b, small_sem.at[k]) for k, (a, b) in enumerate(zip(sources, outs))]
-    for k in range(pieces):
-        copies(k)[0].start()
-    for copy in small:
+    count = (len(refs) - 2) // 2
+    sources, out, outs = refs[:count], refs[count], refs[count + 1 : 2 * count + 1]
+    sem = refs[2 * count + 1]
+    copies = [
+        pltpu.make_async_copy(a, b, sem.at[k]) for k, (a, b) in enumerate(zip((spins, *sources), (out, *outs)))
+    ]
+    for copy in copies:
         copy.start()
-    for k in range(pieces):
-        copies(k)[0].wait()
-        copies(k)[1].start()
-    for k in range(pieces):
-        copies(k)[1].wait()
-    for copy in small:
+    for copy in copies:
         copy.wait()
 
 
@@ -416,6 +417,7 @@
     _, rows, cols = spins_in.shape
     T = rows // H
     f32 = jnp.float32
+    limit = VMEM_BYTES - 4 * rows * cols
     hbm = pl.BlockSpec(memory_space=pltpu.HBM)
     smem = pl.BlockSpec(memory_space=pltpu.SMEM)
     vmem = pl.BlockSpec(memory_space=pltpu.VMEM)
@@ -424,7 +426,7 @@
     results = pl.pallas_call(
         functools.partial(kernel, n, peers, total_rows),
         out_shape=(
-            jax.ShapeDtypeStruct(spins_in.shape, f32),
+            pltpu.VMEM(spins_in.shape, f32),
             jax.ShapeDtypeStruct((1, rows), f32),
             jax.ShapeDtypeStruct((1, rows), f32),
             jax.ShapeDtypeStruct((1,), jnp.int32),
@@ -432,13 +434,13 @@
             jax.ShapeDtypeStruct((1,), f32),
         ),
         in_specs=[hbm, hbm, hbm, smem, hbm],
-        out_specs=(hbm, vmem, vmem, smem, smem, smem),
+        out_specs=(vmem, vmem, vmem, smem, smem, smem),
         scratch_shapes=[
             pltpu.VMEM((T + 2, H, cols), f32),
             pltpu.VMEM((SWEEPS, T + 2, H, cols), jnp.bfloat16),
             pltpu.VMEM((n, T, H, cols // n), f32),
-            pltpu.VMEM((2, SWEEPS, HALO, cols), f32),
-            pltpu.VMEM((2, SWEEPS, HALO, cols), f32),
+            pltpu.VMEM((2, SWEEPS, H, cols), f32),
+            pltpu.VMEM((2, SWEEPS, H, cols), f32),
             pltpu.VMEM((T, H, LANES), f32),
             pltpu.VMEM((n, T, H, LANES), f32),
             pltpu.VMEM((n, 8, rows), f32),
@@ -451,11 +453,10 @@
             pltpu.SMEM(accept.shape, jnp.int32),
             dma((T,)),
             dma((SWEEPS, T)),
-            dma((T,)),
             dma((2, 1 + SWEEPS)),
             dma((2, 1 + SWEEPS)),
-            dma((T, n)),
-            dma((n, T)),
+            dma((T // GROUP, n)),
+            dma((n, T // GROUP)),
             dma((n,)),
             dma((n,)),
             dma((peers,)),
@@ -464,21 +465,16 @@
             dma((n,)),
             dma((2,)),
         ],
-        compiler_params=pltpu.CompilerParams(collective_id=0, has_side_effects=True),
+        compiler_params=pltpu.CompilerParams(collective_id=0, has_side_effects=True, vmem_limit_bytes=limit),
         name="lattice_exchange",
     )(spins_in, noise, betas, labels, accept)
-    pieces = 8
     return pl.pallas_call(
         settle,
         out_shape=tuple(jax.ShapeDtypeStruct(x.shape, x.dtype) for x in results),
-        in_specs=[hbm] * len(results),
+        in_specs=[vmem] + [hbm] * (len(results) - 1),
         out_specs=(hbm,) * len(results),
-        scratch_shapes=[
-            pltpu.VMEM((pieces, rows // pieces, cols), f32),
-            dma((pieces,)),
-            dma((pieces,)),
-            dma((len(results) - 1,)),
-        ],
+        scratch_shapes=[dma((len(results),))],
+        compiler_params=pltpu.CompilerParams(vmem_limit_bytes=VMEM_BYTES // 2),
         name="settle",
     )(*results)
 

time: 71.7 us -> 70.3 us (0.980)
  Pallas kernels: 70.2 us -> 67.5 us
  local copies, waits for them, and re-layouts: 0 us -> 1.29 us
    pallas_call x1, Pallas kernels: 5.43 us -> 3.94 us  [body(): pl.pallas_call(settle, out_shape=tuple((jax.ShapeDtypeStruct(x.shape, x.d...]
    unnamed x0 -> x4, local copies, waits for them, and re-layouts: none -> 1.29 us
    pallas_call x1, Pallas kernels: 64.8 us -> 63.6 us  [body(): pl.pallas_call(functools.partial(kernel, n, peers, total_rows), out_shape...]
where the time goes in v3:
time: 70.3 us; the launch traced here: 70.1 us
  Pallas kernels  67.5 us (96%)
  between operations  1.3 us (2%)
  local copies, waits for them, and re-layouts  1.29 us (2%)
    pallas_call x1, Pallas kernels, body(): pl.pallas_call(functools.partial(kernel, n, peers, total_rows), out_shape...  63.6 us
    pallas_call x1, Pallas kernels, body(): pl.pallas_call(settle, out_shape=tuple((jax.ShapeDtypeStruct(x.shape, x.d...  3.94 us

profile of v3, /device:TPU:0, one launch (start us, length us, event | category | flops | bytes accessed | tf_op | source)
XLA Modules:
  0.0 70.1 jit_solution(3862504926840203667)
XLA Ops:
  1.3 63.6 %lattice_exchange.1 = (f32[1,256,4096]{2,1,0:T(8,128)S(1)}, f32[1,256]{1,0:T(1,128)}, f32[1,256]{1,0:T(1,128)}, s32[1]{0:T(128)}, f32[1]{0:T(128)}, /*index=5*/f32[1]{0:T(128)}) custom-call(f32[1,256,4096]{2,1,0:T(8,128)} %spins_ref.1, bf16[2,1,256,4096]{3,2,1,0:T(8,128)(2,1)} %noise_ref.1, f32[4]{0:T(128)} %betas_hbm.1, s32[1]{0:T(128)S(6)} %copy.11.labels_ref, ...), custom_call_target="tpu_custom_call" | custom-call | tf_op jit(solution)/shard_map/lattice_exchange/pallas_call | solution.py:426
  64.9 0.0 copy-start
  64.9 0.7 copy-done
  65.6 0.0 copy-start.1
  65.6 0.6 copy-done.1
  66.2 3.9 %settle.1 = (f32[1,256,4096]{2,1,0:T(8,128)}, f32[1,256]{1,0:T(1,128)}, f32[1,256]{1,0:T(1,128)}, s32[1]{0:T(128)}, f32[1]{0:T(128)}, /*index=5*/f32[1]{0:T(128)}) custom-call(f32[1,256,4096]{2,1,0:T(8,128)S(1)} %get-tuple-element.12.spins, f32[1,256]{1,0:T(1,128)S(1)} %copy-done, f32[1,256]{1,0:T(1,128)S(1)} %copy-done.1, s32[1]{0:T(128)} %get-tuple-element.15.refs_2_, ...), custom_call_target="tpu_custom_call" | custom-call | tf_op jit(solution)/shard_map/settle/pallas_call | solution.py:471
Async XLA Ops:
  64.9 0.7 copy-start
  65.6 0.6 copy-start.1

commit v4 on v3

--- a/solution.py
+++ b/solution.py
@@ -11,6 +11,7 @@
 H = 8
 GROUP = 2
 LANES = 128
+PIECES = 8
 VMEM_BYTES = 60 * 1024 * 1024
 STAGES = 2 * SWEEPS
 MESH = pl.DeviceIdType.MESH
@@ -39,14 +40,14 @@
 def kernel(
     n, peers, total_rows,
     spins_ref, noise_ref, betas_hbm, labels_ref, accept_hbm,
-    out_ref, energy_ref, margin_ref, label_out, log_out, beta_out,
+    out_ref, energy_ref, margin_ref, small_ref,
     S, N, R, NH, NR, EP, MP, MS, MR, EM, EG, LM, LG, betas_ref, accept_ref,
     s_sem, n_sem, hs_sem, hr_sem, bs_sem, br_sem,
     ms_sem, mr_sem, es_sem, er_sem, ls_sem, lr_sem, i_sem,
 ):
     _, rows, cols = spins_ref.shape
     T = rows // H
-    width = min(1024, cols)
+    width = min(4096, cols)
     share = cols // n
     me = lax.axis_index("rep")
     tile = lax.axis_index("tile")
@@ -141,10 +142,9 @@
         for b in range(cols // width):
             c0 = b * width
             cs = slice(c0, c0 + width)
-            ext = with_sides(S, i, c0, width, cols)
-            cur = ext[:, LANES : LANES + width]
-            left = pltpu.roll(ext, 1, 1)[:, LANES : LANES + width]
-            right = pltpu.roll(ext, width + 2 * LANES - 1, 1)[:, LANES : LANES + width]
+            cur = S[i, :, cs]
+            left = pltpu.roll(cur, 1, 1)
+            right = pltpu.roll(cur, cols - 1, 1)
             up = jnp.where(row == 0, S[above, H - 1 : H, cs], pltpu.roll(cur, 1, 0))
             down = jnp.where(row == H - 1, S[below, 0:1, cs], pltpu.roll(cur, H - 1, 0))
             field = (up + down) + (left + right)
@@ -237,9 +237,6 @@
     def _(t):
         finish(t)
 
-    @pl.loop(0, STAGES // GROUP)
-    def _(p):
-        send(p)
 
     per_row = jnp.sum(EP[...].reshape(rows, LANES).T, axis=0, keepdims=True) * (-1.0 / cols)
     energy_ref[...] = per_row
@@ -295,6 +292,10 @@
     def _(d):
         ladder_copy(d).start()
 
+    @pl.loop(0, STAGES // GROUP)
+    def _(p):
+        send(p)
+
     def bulk_from(d, p):
         src = lax.rem(me + d, n)
         return pltpu.make_async_remote_copy(
@@ -302,9 +303,7 @@
             bs_sem.at[0, 1], br_sem.at[src, p], device_id={"rep": src}, device_id_type=MESH,
         )
 
-    @pl.loop(STAGES // GROUP, (T + STAGES) // GROUP)
-    def _(s):
-        p = lax.rem(s, T // GROUP)
+    def margins(p):
         for d in range(1, n):
             bulk_from(d, p).wait_recv()
         for g in range(GROUP):
@@ -318,25 +317,19 @@
             for r in range(n):
                 MP[r, t] = totals[r]
 
-    for r in range(n):
-        sums = jnp.sum(MP[r].reshape(rows, LANES).T, axis=0, keepdims=True)
-        MS[r] = jnp.broadcast_to(sums, (8, rows))
-    MR[me] = MS[me]
-
-    def margin_copy(d):
-        dest = lax.rem(me + d, n)
-        return pltpu.make_async_remote_copy(
-            MS.at[dest], MR.at[me], ms_sem.at[d], mr_sem.at[me], device_id={"rep": dest}, device_id_type=MESH
-        )
-
-    def margin_from(d):
-        src = lax.rem(me + d, n)
-        return pltpu.make_async_remote_copy(
-            MS.at[0], MR.at[src], ms_sem.at[d], mr_sem.at[src], device_id={"rep": src}, device_id_type=MESH
-        )
-
-    for d in range(1, n):
-        margin_copy(d).start()
+    def margin_sums(first, last):
+        for r in range(n):
+            part = MP[r, first:last].reshape((last - first) * H, LANES)
+            sums = jnp.sum(part.T, axis=0, keepdims=True)
+            MS[r, :, first * H : last * H] = jnp.broadcast_to(sums, (8, (last - first) * H))
+
+    @pl.loop(STAGES // GROUP, T // GROUP)
+    def _(p):
+        margins(p)
+
+    split = LANES // H
+    if split < T:
+        margin_sums(split, T)
 
     @pl.loop(1, n)
     def _(d):
@@ -376,9 +369,29 @@
         my_label = jnp.where(me == r, labels_two[r], my_label)
         my_log = jnp.where(me == r, log, my_log)
         my_beta = jnp.where(me == r, two[r], my_beta)
-    label_out[0] = jnp.max(my_label).astype(jnp.int32)
-    log_out[0] = jnp.max(my_log)
-    beta_out[0] = jnp.max(my_beta)
+    small_ref[...] = jnp.concatenate([my_label, my_log, my_beta, jnp.zeros((5, LANES), jnp.float32)], axis=0)
+
+    @pl.loop(0, STAGES // GROUP)
+    def _(p):
+        margins(p)
+
+    margin_sums(0, min(split, T))
+    MR[me] = MS[me]
+
+    def margin_copy(d):
+        dest = lax.rem(me + d, n)
+        return pltpu.make_async_remote_copy(
+            MS.at[dest], MR.at[me], ms_sem.at[d], mr_sem.at[me], device_id={"rep": dest}, device_id_type=MESH
+        )
+
+    def margin_from(d):
+        src = lax.rem(me + d, n)
+        return pltpu.make_async_remote_copy(
+            MS.at[0], MR.at[src], ms_sem.at[d], mr_sem.at[src], device_id={"rep": src}, device_id_type=MESH
+        )
+
+    for d in range(1, n):
+        margin_copy(d).start()
 
     for copy in halos:
         copy.wait_send()
@@ -400,14 +413,22 @@
     margin_ref[...] = jnp.sum(MR[...], axis=0)[0:1] * (1.0 / cols)
 
 
-def settle(spins, *refs):
-    count = (len(refs) - 2) // 2
-    sources, out, outs = refs[:count], refs[count], refs[count + 1 : 2 * count + 1]
-    sem = refs[2 * count + 1]
-    copies = [
-        pltpu.make_async_copy(a, b, sem.at[k]) for k, (a, b) in enumerate(zip((spins, *sources), (out, *outs)))
+def settle(spins, energy, margin, small, *refs):
+    spins_out, energy_out, margin_out, label_out, log_out, beta_out = refs[:6]
+    label, log, beta, sem = refs[6:]
+    height = spins.shape[1] // PIECES
+    pairs = [(energy, energy_out), (margin, margin_out)]
+    pairs += [
+        (spins.at[0, pl.ds(k * height, height)], spins_out.at[0, pl.ds(k * height, height)]) for k in range(PIECES)
     ]
-    for copy in copies:
+    pairs += [(label, label_out), (log, log_out), (beta, beta_out)]
+    copies = [pltpu.make_async_copy(a, b, sem.at[k]) for k, (a, b) in enumerate(pairs)]
+    for copy in copies[:-3]:
+        copy.start()
+    label[0] = jnp.max(small[0:1]).astype(jnp.int32)
+    log[0] = jnp.max(small[1:2])
+    beta[0] = jnp.max(small[2:3])
+    for copy in copies[-3:]:
         copy.start()
     for copy in copies:
         copy.wait()
@@ -417,7 +438,7 @@
     _, rows, cols = spins_in.shape
     T = rows // H
     f32 = jnp.float32
-    limit = VMEM_BYTES - 4 * rows * cols
+    limit = VMEM_BYTES - 4 * (rows * cols + 2 * rows + 8 * LANES)
     hbm = pl.BlockSpec(memory_space=pltpu.HBM)
     smem = pl.BlockSpec(memory_space=pltpu.SMEM)
     vmem = pl.BlockSpec(memory_space=pltpu.VMEM)
@@ -427,14 +448,12 @@
         functools.partial(kernel, n, peers, total_rows),
         out_shape=(
             pltpu.VMEM(spins_in.shape, f32),
-            jax.ShapeDtypeStruct((1, rows), f32),
-            jax.ShapeDtypeStruct((1, rows), f32),
-            jax.ShapeDtypeStruct((1,), jnp.int32),
-            jax.ShapeDtypeStruct((1,), f32),
-            jax.ShapeDtypeStruct((1,), f32),
+            pltpu.VMEM((1, rows), f32),
+            pltpu.VMEM((1, rows), f32),
+            pltpu.VMEM((8, LANES), f32),
         ),
         in_specs=[hbm, hbm, hbm, smem, hbm],
-        out_specs=(vmem, vmem, vmem, smem, smem, smem),
+        out_specs=(vmem,) * 4,
         scratch_shapes=[
             pltpu.VMEM((T + 2, H, cols), f32),
             pltpu.VMEM((SWEEPS, T + 2, H, cols), jnp.bfloat16),
@@ -470,10 +489,22 @@
     )(spins_in, noise, betas, labels, accept)
     return pl.pallas_call(
         settle,
-        out_shape=tuple(jax.ShapeDtypeStruct(x.shape, x.dtype) for x in results),
-        in_specs=[vmem] + [hbm] * (len(results) - 1),
-        out_specs=(hbm,) * len(results),
-        scratch_shapes=[dma((len(results),))],
+        out_shape=(
+            jax.ShapeDtypeStruct(spins_in.shape, f32),
+            jax.ShapeDtypeStruct((1, rows), f32),
+            jax.ShapeDtypeStruct((1, rows), f32),
+            jax.ShapeDtypeStruct((1,), jnp.int32),
+            jax.ShapeDtypeStruct((1,), f32),
+            jax.ShapeDtypeStruct((1,), f32),
+        ),
+        in_specs=[vmem] * 4,
+        out_specs=(hbm,) * 6,
+        scratch_shapes=[
+            pltpu.SMEM((1,), jnp.int32),
+            pltpu.SMEM((1,), f32),
+            pltpu.SMEM((1,), f32),
+            dma((PIECES + 5,)),
+        ],
         compiler_params=pltpu.CompilerParams(vmem_limit_bytes=VMEM_BYTES // 2),
         name="settle",
     )(*results)

time: 70.3 us -> 63.8 us (0.908)
  Pallas kernels: 67.5 us -> 62.3 us
  local copies, waits for them, and re-layouts: 1.29 us -> 0 us
    pallas_call x1, Pallas kernels: 63.6 us -> 60.2 us  [body(): pl.pallas_call(functools.partial(kernel, n, peers, total_rows), out_shape...]
    pallas_call x1, Pallas kernels: 3.94 us -> 2.15 us  [body(): pl.pallas_call(settle, out_shape=(jax.ShapeDtypeStruct(spins_in.shape, f3...]
    unnamed x4 -> x0, local copies, waits for them, and re-layouts: 1.29 us -> none
where the time goes in v4:
time: 63.8 us; the launch traced here: 63.6 us
  Pallas kernels  62.3 us (98%)
  between operations  1.29 us (2%)
    pallas_call x1, Pallas kernels, body(): pl.pallas_call(functools.partial(kernel, n, peers, total_rows), out_shape...  60.2 us
    pallas_call x1, Pallas kernels, body(): pl.pallas_call(settle, out_shape=(jax.ShapeDtypeStruct(spins_in.shape, f3...  2.15 us

profile of v4, /device:TPU:0, one launch (start us, length us, event | category | flops | bytes accessed | tf_op | source)
XLA Modules:
  0.0 63.6 jit_solution(16974324589536822975)
XLA Ops:
  1.3 60.2 %lattice_exchange.1 = (f32[1,256,4096]{2,1,0:T(8,128)S(1)}, f32[1,256]{1,0:T(1,128)S(1)}, f32[1,256]{1,0:T(1,128)S(1)}, f32[8,128]{1,0:T(8,128)S(1)}) custom-call(f32[1,256,4096]{2,1,0:T(8,128)} %spins_ref.1, bf16[2,1,256,4096]{3,2,1,0:T(8,128)(2,1)} %noise_ref.1, f32[4]{0:T(128)} %betas_hbm.1, s32[1]{0:T(128)S(6)} %copy.11.labels_ref, s32[1,2]{1,0:T(1,128)} %bitcast.1), custom_call_target="tpu_custom_call" | custom-call | tf_op jit(solution)/shard_map/lattice_exchange/pallas_call | solution.py:447
  61.5 2.2 %settle.1 = (f32[1,256,4096]{2,1,0:T(8,128)}, f32[1,256]{1,0:T(1,128)}, f32[1,256]{1,0:T(1,128)}, s32[1]{0:T(128)}, f32[1]{0:T(128)}, /*index=5*/f32[1]{0:T(128)}) custom-call(f32[1,256,4096]{2,1,0:T(8,128)S(1)} %get-tuple-element.10.spins, f32[1,256]{1,0:T(1,128)S(1)} %get-tuple-element.11.energy, f32[1,256]{1,0:T(1,128)S(1)} %get-tuple-element.12.margin, ...), custom_call_target="tpu_custom_call" | custom-call | tf_op jit(solution)/shard_map/settle/pallas_call | solution.py:490
